TPU v7x, 32 devices: a whole 2x2x4 slice. The times are simulated.
32 devices in a mesh: dp: 8 (over z, x), ctx: 4 (over y, core).
Axes of the slice: x: 2, y: 2, z: 4, core: 2. Of those that a mesh axis runs over, the one named last changes fastest.
Arguments:
- tokens: bfloat16 [8192, 1536], P(('dp', 'ctx')), may hold values from -6 to 6
- norm_attn: float32 [1536], P(('dp', 'ctx')), may hold values from 0.5 to 1.5
- w_qkv: bfloat16 [3072, 1536], P(('dp', 'ctx')), may hold values from -1 to 1
- w_out: bfloat16 [1536, 1536], P(('dp', 'ctx')), may hold values from -0.875 to 0.875
- norm_mlp: float32 [1536], P(('dp', 'ctx')), may hold values from 0.5 to 1.5
- w_gate_up: bfloat16 [8192, 1536], P(('dp', 'ctx')), may hold values from -0.15625 to 0.15625
- w_down: bfloat16 [1536, 4096], P(('dp', 'ctx')), may hold values from -0.09375 to 0.09375
- cotangent: bfloat16 [8192, 1536], P(('dp', 'ctx')), may hold values from -6 to 6
- seq_lengths: int32 [8, 2], P('dp'), may hold values from 1 to 768, 1024 in all within a row
- block_slot: int32 [8, 8], P('dp'), may hold values from 0 to 7, each once within a row
Outputs:
- result: bfloat16 [8192, 1536], P(('dp', 'ctx'))
- grad_input: float32 [8192, 1536], P(('dp', 'ctx'))
- grad_norm_attn: float32 [1536], P(('dp', 'ctx'))
- grad_qkv: float32 [3072, 1536], P(('dp', 'ctx'))
- grad_out: float32 [1536, 1536], P(('dp', 'ctx'))
- grad_norm_mlp: float32 [1536], P(('dp', 'ctx'))
- grad_gate_up: float32 [8192, 1536], P(('dp', 'ctx'))
- grad_down: float32 [1536, 4096], P(('dp', 'ctx'))
Inputs may be any that keep to these rules, and one draw needn't show every extreme that they name: `seq_lengths`: each row sums to 1024. `block_slot`: each row names every number once; ctx device c of group g holds the blocks of positions c * 2 to (c + 1) * 2 - 1 of that row.
All inputs are finite; a program needn't handle non-finite values.
Results may differ from a plain program's by a relative error of at most 0.025.
Values may be sent and summed in bfloat16 or wider, within the bound.
A program may use at most 320 MiB of HBM per device.

v0:
```python
import math
import jax
import jax.numpy as jnp
from jax import lax
from jax.sharding import PartitionSpec as P

QUERY_HEADS = 16
KEY_VALUE_HEADS = 8
HEAD_SIZE = 96
FF = 4096
BLK = 128
QUERY_FEATURES = 1536
KEY_FEATURES = 768
EPSILON = 1e-05
THETA = 100000.0
MASK_FILL = -1e30


def rope_tables(rope_pos):
    half_dim = HEAD_SIZE // 2
    exponent = jnp.arange(half_dim, dtype=jnp.float32) * (2.0 / HEAD_SIZE)
    frequency = jnp.power(jnp.float32(THETA), -exponent)
    angles = rope_pos.astype(jnp.float32)[:, None] * frequency[None, :]
    return (jnp.cos(angles)[:, None, :], jnp.sin(angles)[:, None, :])


def apply_rotation(values, cosine_table, sine_values):
    half_dim = HEAD_SIZE // 2
    first_half = values[..., :half_dim]
    second_half = values[..., half_dim:]
    return jnp.concatenate(
        [
            first_half * cosine_table - second_half * sine_values,
            second_half * cosine_table + first_half * sine_values,
        ],
        -1,
    )


def rotate_back(gradient, cosine_table, sine_values):
    half_dim = HEAD_SIZE // 2
    first_half = gradient[..., :half_dim]
    second_half = gradient[..., half_dim:]
    return jnp.concatenate(
        [
            first_half * cosine_table + second_half * sine_values,
            second_half * cosine_table - first_half * sine_values,
        ],
        -1,
    )


def positions(lengths, slot_table, first_row, count_of_rows):
    row_index = first_row + jnp.arange(count_of_rows, dtype=jnp.int32)
    block_index = row_index // BLK
    lookup = jnp.arange(slot_table.shape[0], dtype=jnp.int32)
    slot_of = jnp.sum(jnp.where(block_index[:, None] == lookup[None, :], slot_table[None, :], 0), 1)
    stream = slot_of * BLK + row_index % BLK
    seq_ends = jnp.cumsum(lengths)
    passed = stream[:, None] >= seq_ends[None, :]
    segment = jnp.sum(passed.astype(jnp.int32), 1)
    offset = jnp.sum(jnp.where(passed, seq_ends[None, :], 0), 1)
    return (stream, segment, stream - offset)


def norm_back(grad_normed, gain, source, scale):
    weighted = grad_normed * gain
    return scale * weighted - source * scale**3 * jnp.mean(weighted * source, -1, keepdims=True)


def full_product(left_side, whole_weight):
    return jnp.dot(left_side, whole_weight.T, preferred_element_type=jnp.float32)


def full_back(grad_side, whole_weight):
    return jnp.dot(grad_side, whole_weight, preferred_element_type=jnp.float32)


def owned_three(first_part, second_part, third_part):
    return (
        lax.psum_scatter(first_part, ("dp", "ctx"), scatter_dimension=0, tiled=True),
        lax.psum_scatter(second_part, ("dp", "ctx"), scatter_dimension=0, tiled=True),
        lax.psum_scatter(third_part, ("dp", "ctx"), scatter_dimension=0, tiled=True),
    )


def shards(
    tokens, norm_attn, w_qkv, w_out, norm_mlp, w_gate_up, w_down, cotangent, seq_lengths, block_slot
):
    count_of_rows = tokens.shape[0]
    ctx_place = lax.axis_index("ctx")
    lengths = seq_lengths[0]
    slot_table = block_slot[0]
    heads_ratio = QUERY_HEADS // KEY_VALUE_HEADS
    score_scale = 1.0 / math.sqrt(HEAD_SIZE)
    stream, segment, rope_pos = positions(
        lengths, slot_table, ctx_place * count_of_rows, count_of_rows
    )
    cosine_table, sine_values = rope_tables(rope_pos)
    gain_one, gain_two = (
        lax.all_gather(norm_attn, ("dp", "ctx"), axis=0, tiled=True),
        lax.all_gather(norm_mlp, ("dp", "ctx"), axis=0, tiled=True),
    )
    qkv_full, out_full = (
        lax.all_gather(w_qkv, ("dp", "ctx"), axis=0, tiled=True),
        lax.all_gather(w_out, ("dp", "ctx"), axis=0, tiled=True),
    )
    source = tokens.astype(jnp.float32)
    scale_one = lax.rsqrt(jnp.mean(source * source, -1, keepdims=True) + EPSILON)
    normed_one = (source * scale_one * gain_one).astype(jnp.bfloat16)
    projected_output = full_product(normed_one, qkv_full)
    query_rows = apply_rotation(
        projected_output[:, :QUERY_FEATURES].reshape(count_of_rows, QUERY_HEADS, HEAD_SIZE),
        cosine_table,
        sine_values,
    ).astype(jnp.bfloat16)
    keys_mine = apply_rotation(
        projected_output[:, QUERY_FEATURES : QUERY_FEATURES + KEY_FEATURES].reshape(
            count_of_rows, KEY_VALUE_HEADS, HEAD_SIZE
        ),
        cosine_table,
        sine_values,
    ).astype(jnp.bfloat16)
    values_mine = projected_output[:, QUERY_FEATURES + KEY_FEATURES :].astype(jnp.bfloat16)
    grouped_queries = query_rows.reshape(count_of_rows, KEY_VALUE_HEADS, heads_ratio, HEAD_SIZE)
    key_value = jnp.concatenate([keys_mine.reshape(count_of_rows, KEY_FEATURES), values_mine], 1)

    def masked(block_portion, start_row):
        portion_rows = block_portion.shape[0]
        key_stream, key_segment, unused = positions(lengths, slot_table, start_row, portion_rows)
        key_portion = block_portion[:, :KEY_FEATURES].reshape(
            portion_rows, KEY_VALUE_HEADS, HEAD_SIZE
        )
        value_portion = block_portion[:, KEY_FEATURES:].reshape(
            portion_rows, KEY_VALUE_HEADS, HEAD_SIZE
        )
        scores = (
            jnp.einsum(
                "rgjd,ngd->gjrn", grouped_queries, key_portion, preferred_element_type=jnp.float32
            )
            * score_scale
        )
        allowed = (
            (segment[:, None] == key_segment[None, :]) & (key_stream[None, :] <= stream[:, None])
        )[None, None]
        return (jnp.where(allowed, scores, MASK_FILL), allowed, key_portion, value_portion)

    highest_score = jnp.full((KEY_VALUE_HEADS, heads_ratio, count_of_rows), MASK_FILL, jnp.float32)
    scores, allowed, key_portion, value_portion = masked(
        lax.all_gather(key_value, "ctx", axis=0, tiled=True), jnp.int32(0)
    )
    new_high = jnp.maximum(highest_score, jnp.max(scores, -1))
    weights = jnp.where(allowed, jnp.exp(scores - new_high[..., None]), 0.0)
    weight_sum = jnp.sum(weights, -1)
    gained = jnp.einsum(
        "gjrn,ngd->rgjd",
        weights.astype(jnp.bfloat16),
        value_portion,
        preferred_element_type=jnp.float32,
    )
    accumulated = gained
    highest_score, weight_sum, accumulated = (new_high, weight_sum, accumulated)
    log_total = highest_score + jnp.log(weight_sum)
    attention_output = (
        (accumulated / jnp.transpose(weight_sum, (2, 0, 1))[..., None])
        .astype(jnp.bfloat16)
        .reshape(count_of_rows, QUERY_FEATURES)
    )
    residual = source + full_product(attention_output, out_full)
    scale_two = lax.rsqrt(jnp.mean(residual * residual, -1, keepdims=True) + EPSILON)
    normed_two = (residual * scale_two * gain_two).astype(jnp.bfloat16)
    gate_up_full, down_full = (
        lax.all_gather(w_gate_up, ("dp", "ctx"), axis=0, tiled=True),
        lax.all_gather(w_down, ("dp", "ctx"), axis=0, tiled=True),
    )
    gate_up = full_product(normed_two, gate_up_full)
    gate_part = gate_up[:, :FF]
    up_part = gate_up[:, FF:]
    sigmoid = jax.nn.sigmoid(gate_part)
    hidden = (gate_part * sigmoid * up_part).astype(jnp.bfloat16)
    mlp_term = full_product(hidden, down_full)
    result = (residual + mlp_term).astype(jnp.bfloat16)
    gate_up_full, down_full = (
        lax.all_gather(w_gate_up, ("dp", "ctx"), axis=0, tiled=True),
        lax.all_gather(w_down, ("dp", "ctx"), axis=0, tiled=True),
    )
    grad_hidden = full_back(cotangent, down_full)
    grad_down = jnp.dot(cotangent.T, hidden, preferred_element_type=jnp.float32)
    grad_gate = grad_hidden * up_part * sigmoid * (1.0 + gate_part * (1.0 - sigmoid))
    grad_upper = grad_hidden * gate_part * sigmoid
    grad_gu = jnp.concatenate([grad_gate, grad_upper], 1).astype(jnp.bfloat16)
    grad_normed_two = full_back(grad_gu, gate_up_full)
    grad_w_gate_up = jnp.dot(grad_gu.T, normed_two, preferred_element_type=jnp.float32)
    grad_gain_two = jnp.sum(grad_normed_two * residual * scale_two, 0)
    mlp_owned = owned_three(grad_gain_two, grad_w_gate_up, grad_down)
    grad_residual = cotangent.astype(jnp.float32) + norm_back(
        grad_normed_two, gain_two, residual, scale_two
    )
    grad_res_bf = grad_residual.astype(jnp.bfloat16)
    qkv_full, out_full = (
        lax.all_gather(w_qkv, ("dp", "ctx"), axis=0, tiled=True),
        lax.all_gather(w_out, ("dp", "ctx"), axis=0, tiled=True),
    )
    attention_gradient = full_back(grad_res_bf, out_full).astype(jnp.bfloat16)
    grad_w_out = jnp.dot(grad_res_bf.T, attention_output, preferred_element_type=jnp.float32)
    keys_values_all = lax.all_gather(key_value, "ctx", axis=0, tiled=True)
    grouped_gradient = attention_gradient.reshape(
        count_of_rows, KEY_VALUE_HEADS, heads_ratio, HEAD_SIZE
    )
    attention_grouped = attention_output.reshape(
        count_of_rows, KEY_VALUE_HEADS, heads_ratio, HEAD_SIZE
    )
    row_delta = jnp.transpose(
        jnp.sum(grouped_gradient.astype(jnp.float32) * attention_grouped.astype(jnp.float32), -1),
        (1, 2, 0),
    )
    grouped_rows = keys_values_all.shape[0]
    block_rows = min(512, grouped_rows)
    block_count = grouped_rows // block_rows

    def key_block(grad_queries, which_block):
        start_row = which_block * block_rows
        block_portion = lax.dynamic_slice_in_dim(keys_values_all, start_row, block_rows, 0)
        scores, allowed, key_portion, value_portion = masked(block_portion, start_row)
        weights = jnp.where(allowed, jnp.exp(scores - log_total[..., None]), 0.0)
        grad_values = jnp.einsum(
            "gjrn,rgjd->ngd",
            weights.astype(jnp.bfloat16),
            grouped_gradient,
            preferred_element_type=jnp.float32,
        )
        grad_weights = jnp.einsum(
            "rgjd,ngd->gjrn", grouped_gradient, value_portion, preferred_element_type=jnp.float32
        )
        grad_scores = (weights * (grad_weights - row_delta[..., None])).astype(jnp.bfloat16)
        grad_queries = (
            grad_queries
            + jnp.einsum(
                "gjrn,ngd->rgjd", grad_scores, key_portion, preferred_element_type=jnp.float32
            )
            * score_scale
        )
        grad_keys = (
            jnp.einsum(
                "gjrn,rgjd->ngd", grad_scores, grouped_queries, preferred_element_type=jnp.float32
            )
            * score_scale
        )
        return (
            grad_queries,
            jnp.concatenate(
                [
                    grad_keys.reshape(block_rows, KEY_FEATURES),
                    grad_values.reshape(block_rows, KEY_FEATURES),
                ],
                1,
            ),
        )

    grad_queries, key_terms = lax.scan(
        key_block,
        jnp.zeros((count_of_rows, KEY_VALUE_HEADS, heads_ratio, HEAD_SIZE), jnp.float32),
        jnp.arange(block_count, dtype=jnp.int32),
    )
    key_value_gradient = lax.psum_scatter(
        key_terms.reshape(grouped_rows, 2 * KEY_FEATURES).astype(jnp.bfloat16),
        "ctx",
        scatter_dimension=0,
        tiled=True,
    ).astype(jnp.float32)
    grad_queries = rotate_back(
        grad_queries.reshape(count_of_rows, QUERY_HEADS, HEAD_SIZE), cosine_table, sine_values
    ).reshape(count_of_rows, QUERY_FEATURES)
    grad_keys = rotate_back(
        key_value_gradient[:, :KEY_FEATURES].reshape(count_of_rows, KEY_VALUE_HEADS, HEAD_SIZE),
        cosine_table,
        sine_values,
    ).reshape(count_of_rows, KEY_FEATURES)
    grad_projected = jnp.concatenate(
        [grad_queries, grad_keys, key_value_gradient[:, KEY_FEATURES:]], 1
    ).astype(jnp.bfloat16)
    grad_normed_one = full_back(grad_projected, qkv_full)
    grad_w_qkv = jnp.dot(grad_projected.T, normed_one, preferred_element_type=jnp.float32)
    grad_gain_one = jnp.sum(grad_normed_one * source * scale_one, 0)
    grad_tokens = grad_residual + norm_back(grad_normed_one, gain_one, source, scale_one)
    attn_owned = owned_three(grad_gain_one, grad_w_qkv, grad_w_out)
    return (
        result,
        grad_tokens,
        attn_owned[0],
        attn_owned[1],
        attn_owned[2],
        mlp_owned[0],
        mlp_owned[1],
        mlp_owned[2],
    )


def solution(mesh):
    return jax.shard_map(
        shards,
        mesh=mesh,
        in_specs=(
            P(("dp", "ctx"), None),
            P(("dp", "ctx")),
            P(("dp", "ctx"), None),
            P(("dp", "ctx"), None),
            P(("dp", "ctx")),
            P(("dp", "ctx"), None),
            P(("dp", "ctx"), None),
            P(("dp", "ctx"), None),
            P("dp", None),
            P("dp", None),
        ),
        out_specs=(
            P(("dp", "ctx"), None),
            P(("dp", "ctx"), None),
            P(("dp", "ctx")),
            P(("dp", "ctx"), None),
            P(("dp", "ctx"), None),
            P(("dp", "ctx")),
            P(("dp", "ctx"), None),
            P(("dp", "ctx"), None),
        ),
        check_vma=False,
    )
```

profile of v0, /device:TPU:0, one launch (start us, length us, event | category | flops | bytes accessed | tf_op | source)
XLA Modules:
  0.0 1631.1 jit_solution(5330102366979640390)
XLA Ops:
  8.0 0.9 dynamic-update-slice
  8.8 0.9 dynamic-update-slice.1
  9.7 0.8 reduce-window.9
  10.5 43.5 %all-reduce.5 = (f32[1536]{0:T(1024)S(1)}, f32[1536]{0:T(1024)S(1)}) all-reduce(f32[1536]{0:T(1024)S(1)} %dynamic-update-slice, f32[1536]{0:T(1024)S(1)} %dynamic-update-slice.1), channel_id=1, replica_groups=mesh['dp'=8,'ctx'=4] {'dp','ctx'}, use_global_device_ids=true, to_apply=%add | all-reduce | flops 3072 | bytes 24576
  54.9 1.4 fusion.26
  57.1 38.7 %all-gather.6.cloned.1.call-done = bf16[3072,1536]{1,0:T(8,128)(2,1)} async-done(((bf16[96,1536]{1,0:T(8,128)(2,1)}), bf16[3072,1536]{1,0:T(8,128)(2,1)}) %all-gather.6.cloned.1.call-update) | async-done | bytes 9437200 | tf_op jit(solution)/shard_map/all_gather | solution.py:105
  95.9 5.5 fusion.44
  101.4 1.7 copy-done.12
  103.7 0.9 pad_maximum_fusion.4
  107.9 1.6 slice.91
  110.2 1.1 pad_maximum_fusion.5
  111.3 20.5 %all-gather.8.cloned.1.call-done = bf16[1024,1536]{1,0:T(8,128)(2,1)} async-done(((bf16[256,1536]{1,0:T(8,128)(2,1)}), bf16[1024,1536]{1,0:T(8,128)(2,1)}) %all-gather.8.cloned.1.call-update) | async-done | bytes 3145744 | tf_op jit(solution)/shard_map/all_gather | solution.py:150
  131.9 2.1 fusion.69
  134.0 1.6 copy.64
  135.6 0.7 copy.65
  136.4 4.3 fusion.17
  140.7 4.0 fusion.18
  144.8 4.1 fusion.35
  148.9 49.5 %all-gather.10.cloned.1.call-done = bf16[1536,1536]{1,0:T(8,128)(2,1)} async-done(((bf16[48,1536]{1,0:T(8,128)(2,1)}), bf16[1536,1536]{1,0:T(8,128)(2,1)}) %all-gather.10.cloned.1.call-update) | async-done | bytes 4718608 | tf_op jit(solution)/shard_map/all_gather | solution.py:106
  198.4 3.9 multiply_reduce_fusion.3
  202.3 151.2 %all-gather.12.cloned.1.call-done = bf16[8192,1536]{1,0:T(8,128)(2,1)} async-done(((bf16[256,1536]{1,0:T(8,128)(2,1)}), bf16[8192,1536]{1,0:T(8,128)(2,1)}) %all-gather.12.cloned.1.call-update) | async-done | bytes 25165840 | tf_op jit(solution)/shard_map/all_gather | solution.py:173
  353.5 13.7 fusion.66
  367.2 82.5 %all-gather.14.cloned.1.call-done = bf16[1536,4096]{1,0:T(8,128)(2,1)} async-done(((bf16[48,4096]{1,0:T(8,128)(2,1)}), bf16[1536,4096]{1,0:T(8,128)(2,1)}) %all-gather.14.cloned.1.call-update) | async-done | bytes 12582928 | tf_op jit(solution)/shard_map/all_gather | solution.py:174
  449.6 13.2 multiply_convert_fusion.1
  462.9 13.9 multiply_reduce_fusion
  477.2 1.1 copy-done.2
  478.4 1.4 convolution_convert_fusion
  479.8 1.2 copy.68
  480.9 1.4 multiply_reduce_fusion.1
  482.3 59.7 %while.15 = (s32[]{:T(128)}, f32[256,8,2,96]{0,3,2,1:T(8,128)}, bf16[2,512,1536]{2,1,0:T(8,128)(2,1)}, s32[2]{0:T(128)S(1)}, bf16[1024,1536]{1,0:T(8,128)(2,1)},...) while((s32[]{:T(128)}, f32[256,8,2,96]{0,3,2,1:T(8,128)}, ...), condition=%wide.region_16.17_spmd.clone, body=%wide.region_13.16_spmd.clone.sunk | while | flops 2043966464 | bytes 114495864 | solution.py:260
  483.8 1.5 fusion.123
  485.5 5.7 fusion.124
  491.9 6.7 fusion.127
  498.6 4.3 bitcast_add_fusion.2
  502.9 0.9 copy-done.1
  503.8 3.6 fusion.128
  507.4 2.5 bitcast_multiply_fusion.2
  510.8 1.3 constant_dynamic-update-slice_fusion.2
  513.3 1.5 fusion.123
  515.0 5.7 fusion.124
  521.4 6.7 fusion.127
  528.1 4.8 bitcast_add_fusion.2
  532.9 0.9 copy-done.1
  533.8 3.6 fusion.128
  537.4 2.5 bitcast_multiply_fusion.2
  540.7 1.3 constant_dynamic-update-slice_fusion.2
  542.0 4.6 copy.71
  546.8 1.3 copy-done.3
  548.3 6.0 fusion.40
  555.1 1.6 add_convert_fusion
  556.9 26.3 %reduce-scatter.8.cloned.1.call-done = bf16[256,1536]{0,1:T(8,128)(2,1)} async-done(((bf16[1024,1536]{0,1:T(8,128)(2,1)}), bf16[256,1536]{0,1:T(8,128)(2,1)}) %reduce-scatter.8.cloned.1.call-update) | async-done | bytes 786448 | tf_op jit(solution)/shard_map/reduce_scatter | solution.py:265
  583.2 1.2 fusion.70
  585.1 9.6 fusion.38
  594.7 14.9 convolution_bitcast_fusion
  609.6 25.3 %copy.83 = f32[1536,4096]{1,0:T(8,128)} copy(f32[1536,4096]{0,1:T(8,128)} %convolution_bitcast_fusion) | data formatting | bytes 50331648
  635.6 22.7 %fusion.23 = f32[8192,1536]{1,0:T(8,128)} fusion(bf16[256,4096]{1,0:T(8,128)(2,1)} %copy-done.14, bf16[256,4096]{1,0:T(8,128)(2,1)} %copy-done.13, f32[256,1536]{1,0:T(8,128)} %copy-done.6, f32[1536]{0:T(1024)S(1)} %copy-done.25, f32[256]{0:T(256)} %copy-done.30), kind=kOutput, calls=%fused_computation.54 | convolution fusion | flops 6452019200 | bytes 56105984 | tf_op jit(solution)/shard_map/dot_general | solution.py:193
  658.4 10.2 fusion.25
  668.6 8.5 fusion.34
  677.1 41.0 %all-reduce.4 = (f32[1536]{0:T(1024)S(1)}, f32[1536]{0:T(1024)S(1)}) all-reduce(f32[1536]{0:T(1024)} %get-tuple-element.305, f32[1536]{0:T(1024)} %get-tuple-element.303), channel_id=3, replica_groups=mesh['dp'=8,'ctx'=4] {'dp','ctx'}, use_global_device_ids=true, to_apply=%region_20.21.clone | all-reduce | flops 3072 | bytes 24576
  719.9 3.0 fusion.31
  722.9 3.4 reduce-scatter.12.cloned.1.call-done
  726.3 212.8 %reduce-scatter.10.cloned.1.call-done = f32[96,1536]{1,0:T(8,128)} async-done(((f32[3072,1536]{1,0:T(8,128)}), f32[96,1536]{1,0:T(8,128)}) %reduce-scatter.10.cloned.1.call-update) | async-done | bytes 589840 | tf_op jit(solution)/shard_map/reduce_scatter | solution.py:82
  939.1 249.2 %reduce-scatter.16.cloned.1.call-done = f32[48,4096]{1,0:T(8,128)} async-done(((f32[1536,4096]{1,0:T(8,128)}), f32[48,4096]{1,0:T(8,128)}) %reduce-scatter.16.cloned.1.call-update) | async-done | bytes 786448
  1188.3 435.5 %reduce-scatter.14.cloned.1.call-done = f32[256,1536]{1,0:T(8,128)} async-done(((f32[8192,1536]{1,0:T(8,128)}), f32[256,1536]{1,0:T(8,128)}) %reduce-scatter.14.cloned.1.call-update) | async-done | bytes 1572880 | tf_op jit(solution)/shard_map/reduce_scatter | solution.py:82
  (149 shorter events, 16.7 us)
Async XLA Ops:
  7.2 88.7 %all-gather.6.cloned.1.call-start = ((), (), s32[]{:S(2)}) async-start(), calls=%async_computation.5 | async-start | bytes 9732096 | tf_op jit(solution)/shard_map/all_gather | solution.py:105
  7.9 124.0 %all-gather.8.cloned.1.call-start = ((), (), s32[]{:S(2)}) async-start(), calls=%async_computation.6 | async-start | bytes 3932160 | tf_op jit(solution)/shard_map/all_gather | solution.py:150
  54.0 47.3 %copy-start.22 = (f32[1536]{0:T(1024)}, f32[1536]{0:T(1024)S(1)}, u32[]{:S(2)}) copy-start(f32[1536]{0:T(1024)S(1)} %get-tuple-element.337) | copy-start | bytes 18436
  54.0 422.7 %copy-start.24 = (f32[1536]{0:T(1024)}, f32[1536]{0:T(1024)S(1)}, u32[]{:S(2)}) copy-start(f32[1536]{0:T(1024)S(1)} %get-tuple-element.338) | copy-start | bytes 18436
  56.8 44.5 %copy-start.27 = (f32[256]{0:T(256)}, f32[256]{0:T(256)S(1)}, u32[]{:S(2)}) copy-start(f32[256]{0:T(256)S(1)} %get-tuple-element.359) | copy-start | bytes 3076
  57.1 52.8 %copy-start.18 = (f32[256,48]{0,1:T(8,128)}, f32[256,48]{0,1:T(8,128)S(1)}, u32[]{:S(2)}) copy-start(f32[256,48]{0,1:T(8,128)S(1)} %get-tuple-element.356) | copy-start | bytes 147460
  57.1 52.8 %copy-start.20 = (f32[256,48]{0,1:T(8,128)}, f32[256,48]{0,1:T(8,128)S(1)}, u32[]{:S(2)}) copy-start(f32[256,48]{0,1:T(8,128)S(1)} %get-tuple-element.357) | copy-start | bytes 147460
  101.3 1.7 copy-start.12
  103.5 3.7 copy-start.32
  103.5 3.8 copy-start.26
  104.7 93.7 %all-gather.10.cloned.1.call-start = ((), (), s32[]{:S(2)}) async-start(), calls=%async_computation.7 | async-start | bytes 4866048 | tf_op jit(solution)/shard_map/all_gather | solution.py:106
  105.4 248.1 %all-gather.12.cloned.1.call-start = ((), (), s32[]{:S(2)}) async-start(), calls=%async_computation.8 | async-start | bytes 25952256 | tf_op jit(solution)/shard_map/all_gather | solution.py:173
  106.0 343.6 %all-gather.14.cloned.1.call-start = ((), (), s32[]{:S(2)}) async-start(), calls=%async_computation.9 | async-start | bytes 12976128 | tf_op jit(solution)/shard_map/all_gather | solution.py:174
  106.6 476.6 %reduce-scatter.8.cloned.1.call-start = ((), (), s32[]{:S(2)}) async-start(), calls=%async_computation.10 | async-start | bytes 3932160 | tf_op jit(solution)/shard_map/reduce_scatter | solution.py:265
  110.2 1.1 copy-start.7
  110.2 1.1 copy-start.8
  140.7 4.1 copy-start.15
  144.8 53.6 %copy-start.4 = (bf16[256,1536]{1,0:T(8,128)(2,1)S(1)}, bf16[256,1536]{1,0:T(8,128)(2,1)}, u32[]{:S(2)}) copy-start(bf16[256,1536]{1,0:T(8,128)(2,1)} %param.12) | copy-start | bytes 2359300
  148.9 332.0 %copy-start.9 = (bf16[256,8,2,96]{0,3,2,1:T(8,128)(2,1)}, bf16[256,8,2,96]{0,3,2,1:T(8,128)(2,1)S(1)}, u32[]{:S(2)}) copy-start(bf16[256,8,2,96]{0,3,2,1:T(8,128)(2,1)S(1)} %fusion.35) | copy-start | bytes 2359300
  202.2 274.5 %copy-start.6 = (f32[256,1536]{1,0:T(8,128)}, f32[256,1536]{1,0:T(8,128)S(1)}, u32[]{:S(2)}) copy-start(f32[256,1536]{1,0:T(8,128)S(1)} %get-tuple-element.365) | copy-start | bytes 4718596
  202.3 274.5 %copy-start.30 = (f32[256]{0:T(256)}, f32[256]{0:T(256)S(1)}, u32[]{:S(2)}) copy-start(f32[256]{0:T(256)S(1)} %get-tuple-element.361) | copy-start | bytes 3076
  353.5 96.1 %copy-start.11 = (bf16[256,1536]{1,0:T(8,128)(2,1)S(1)}, bf16[256,1536]{1,0:T(8,128)(2,1)}, u32[]{:S(2)}) copy-start(bf16[256,1536]{1,0:T(8,128)(2,1)} %param.19) | copy-start | bytes 2359300
  449.6 28.7 %slice-start = ((s8[4718592]{0:T(1024)(128)(4,1)}), s8[4194304]{0:T(1024)(128)(4,1)S(1)}, s32[]{:S(2)}) async-start(s8[4718592]{0:T(1024)(128)(4,1)} %bitcast.195), calls=%async_computation.15 | async-start | bytes 8388608
  462.9 13.9 copy-start.13
  462.9 13.9 copy-start.14
  462.9 15.5 slice-start.1
  477.2 1.1 copy-start.2
  498.6 5.2 copy-start.1
  503.8 3.6 copy-start
  528.1 5.7 copy-start.1
  533.8 3.6 copy-start
  546.7 1.4 copy-start.3
  546.7 1.6 copy-start.10
  546.7 179.6 %reduce-scatter.12.cloned.1.call-start = ((), (), s32[]{:S(2)}) async-start(), calls=%async_computation.12 | async-start | bytes 9732096 | tf_op jit(solution)/shard_map/reduce_scatter | solution.py:83
  554.3 0.8 copy-start.19
  554.3 0.8 copy-start.21
  554.3 384.8 %reduce-scatter.10.cloned.1.call-start = ((), (), s32[]{:S(2)}) async-start(), calls=%async_computation.11 | async-start | bytes 19464192 | tf_op jit(solution)/shard_map/reduce_scatter | solution.py:82
  556.8 28.3 %copy-start.5 = (bf16[256,1536]{1,0:T(8,128)(2,1)S(1)}, bf16[256,1536]{1,0:T(8,128)(2,1)}, u32[]{:S(2)}) copy-start(bf16[256,1536]{1,0:T(8,128)(2,1)} %param.12) | copy-start | bytes 2359300
  556.8 28.2 %copy-start.23 = (f32[1536]{0:T(1024)S(1)}, f32[1536]{0:T(1024)}, u32[]{:S(2)}) copy-start(f32[1536]{0:T(1024)} %copy-done.22) | copy-start | bytes 18436
  556.9 28.2 %copy-start.28 = (f32[256]{0:T(256)S(1)}, f32[256]{0:T(256)}, u32[]{:S(2)}) copy-start(f32[256]{0:T(256)} %copy-done.27) | copy-start | bytes 3076
  584.3 0.8 copy-start.16
  594.7 593.6 %reduce-scatter.16.cloned.1.call-start = ((), (), s32[]{:S(2)}) async-start(), calls=%async_computation.14 | async-start | bytes 25952256
  634.9 0.7 copy-start.25
  635.0 988.9 %reduce-scatter.14.cloned.1.call-start = ((), (), s32[]{:S(2)}) async-start(), calls=%async_computation.13 | async-start | bytes 51904512 | tf_op jit(solution)/shard_map/reduce_scatter | solution.py:82
  658.4 10.2 copy-start.17
  658.4 10.2 copy-start.29
  668.6 51.4 %copy-start.31 = (f32[256]{0:T(256)S(1)}, f32[256]{0:T(256)}, u32[]{:S(2)}) copy-start(f32[256]{0:T(256)} %get-tuple-element.358) | copy-start | bytes 3076
Sparse Core Ops, SparseCore 0:
  10.9 84.9 all-gather.5
  104.8 27.0 all-gather.7
  134.8 63.5 all-gather.9
  201.1 152.3 all-gather.11
  356.2 93.3 all-gather.13
  546.8 36.2 reduce-scatter.7
  589.6 136.6 reduce-scatter.11
  733.3 205.7 reduce-scatter.9
  946.1 242.1 reduce-scatter.15
  1195.1 428.6 reduce-scatter.13
where the time goes:
time: 1640 us; the launch traced here: 1630 us
  waiting for transfers between devices  1270 us (77%)
  matrix products  178 us (11%)
  blocking collectives  84.6 us (5%)
  local copies, waits for them, and re-layouts  59.6 us (4%)
  other arithmetic  19.4 us (1%)
    reduce_scatter x2, waiting for transfers between devices, owned_three(): lax.psum_scatter(second_part, ('dp', 'ctx'), scatter_dimension=0, tiled=T...  648 us
    unnamed x11, waiting for transfers between devices  252 us
    all_gather x1, waiting for transfers between devices, shards(): lax.all_gather(w_gate_up, ('dp', 'ctx'), axis=0, tiled=True)  151 us
    unnamed x2, blocking collectives  84.6 us
    all_gather x1, waiting for transfers between devices, shards(): lax.all_gather(w_down, ('dp', 'ctx'), axis=0, tiled=True)  82.5 us
    all_gather x1, waiting for transfers between devices, shards(): lax.all_gather(w_out, ('dp', 'ctx'), axis=0, tiled=True)  49.5 us
    all_gather x1, waiting for transfers between devices, shards(): lax.all_gather(w_qkv, ('dp', 'ctx'), axis=0, tiled=True)  38.7 us
    dot_general x4, matrix products, full_back(): return jnp.dot(grad_side, whole_weight, preferred_element_type=jnp.float32)  37 us
  transfers between devices with their start and end apart: 10, of which 10 were waited for; matrix products, arithmetic and copies ran while one was open for 9% of the time, Pallas kernels for 0%

commit v1 on v0

--- a/solution.py
+++ b/solution.py
@@ -14,6 +14,19 @@
 EPSILON = 1e-05
 THETA = 100000.0
 MASK_FILL = -1e30
+
+
+def check_the_stops_all(body, mesh_ax, dim_at):
+    inter = lax.axis_index(mesh_ax)
+    later = lax.axis_size(mesh_ax)
+    local_next, reply, w2 = (later, inter, body.shape[dim_at])
+    known, response = (body, 1)
+    while response < local_next:
+        fresh = tuple(((d, (d - response) % local_next) for d in range(local_next)))
+        b_now = lax.ppermute(known, axis_name=mesh_ax, perm=fresh)
+        known = jnp.concatenate([known, b_now], axis=dim_at)
+        response = 2 * response
+    return jnp.roll(known, reply * w2, dim_at)
 
 
 def rope_tables(rope_pos):
@@ -170,7 +183,7 @@
     scale_two = lax.rsqrt(jnp.mean(residual * residual, -1, keepdims=True) + EPSILON)
     normed_two = (residual * scale_two * gain_two).astype(jnp.bfloat16)
     gate_up_full, down_full = (
-        lax.all_gather(w_gate_up, ("dp", "ctx"), axis=0, tiled=True),
+        check_the_stops_all(w_gate_up, ("dp", "ctx"), 0),
         lax.all_gather(w_down, ("dp", "ctx"), axis=0, tiled=True),
     )
     gate_up = full_product(normed_two, gate_up_full)

time: 1640 us -> 2360 us (1.44)
  waiting for transfers between devices: 1270 us -> 1920 us
  local copies, waits for them, and re-layouts: 59.6 us -> 125 us
    ppermute x0 -> x5, waiting for transfers between devices: none -> 522 us  [check_the_stops_all(): b_now = lax.ppermute(known, axis_name=mesh_ax, perm=fresh)]
    all_gather x1, waiting for transfers between devices: 49.5 us -> 261 us  [shards(): lax.all_gather(w_out, ('dp', 'ctx'), axis=0, tiled=True)]
    reduce_scatter x1, waiting for transfers between devices: 3.36 us -> 142 us  [owned_three(): lax.psum_scatter(third_part, ('dp', 'ctx'), scatter_dimension=0, tiled=True)]
    unnamed x11, waiting for transfers between devices: 252 us -> 135 us
    all_gather x1, waiting for transfers between devices: 82.5 us -> 26 us  [shards(): lax.all_gather(w_down, ('dp', 'ctx'), axis=0, tiled=True)]
    unnamed x73 -> x95, local copies, waits for them, and re-layouts: 34.6 us -> 64 us
    reduce_scatter x1, waiting for transfers between devices: 26.3 us -> 0.02 us  [shards(): lax.psum_scatter(key_terms.reshape(grouped_rows, 2 * KEY_FEATURES).astype...]
  transfers between devices with their start and end apart: 10 -> 15, of which waited for: 10 -> 13; matrix products, arithmetic and copies ran while one was open for 9% -> 9% of each run, Pallas kernels for 0% -> 0%
where the time goes in v1:
time: 2360 us; the launch traced here: 2350 us
  waiting for transfers between devices  1920 us (81%)
  matrix products  175 us (7%)
  local copies, waits for them, and re-layouts  125 us (5%)
  blocking collectives  85 us (4%)
    reduce_scatter x2, waiting for transfers between devices, owned_three(): lax.psum_scatter(second_part, ('dp', 'ctx'), scatter_dimension=0, tiled=T...  648 us
    ppermute x5, waiting for transfers between devices, check_the_stops_all(): b_now = lax.ppermute(known, axis_name=mesh_ax, perm=fresh)  522 us
    all_gather x1, waiting for transfers between devices, shards(): lax.all_gather(w_out, ('dp', 'ctx'), axis=0, tiled=True)  261 us
    reduce_scatter x1, waiting for transfers between devices, owned_three(): lax.psum_scatter(third_part, ('dp', 'ctx'), scatter_dimension=0, tiled=True)  142 us
    all_gather x1, waiting for transfers between devices, shards(): lax.all_gather(w_gate_up, ('dp', 'ctx'), axis=0, tiled=True)  142 us
    unnamed x11, waiting for transfers between devices  135 us
    unnamed x2, blocking collectives  85 us
    unnamed x95, local copies, waits for them, and re-layouts  64 us
  transfers between devices with their start and end apart: 15, of which 13 were waited for; matrix products, arithmetic and copies ran while one was open for 9% of the time, Pallas kernels for 0%

profile of v1, /device:TPU:0, one launch (start us, length us, event | category | flops | bytes accessed | tf_op | source)
XLA Modules:
  0.0 2354.0 jit_solution(6308428788389417193)
XLA Ops:
  10.5 42.7 %all-reduce.5 = (f32[1536]{0:T(1024)S(1)}, f32[1536]{0:T(1024)S(1)}) all-reduce(f32[1536]{0:T(1024)S(1)} %dynamic-update-slice, f32[1536]{0:T(1024)S(1)} %dynamic-update-slice.1), channel_id=1, replica_groups=mesh['dp'=8,'ctx'=4] {'dp','ctx'}, use_global_device_ids=true, to_apply=%add | all-reduce | flops 3072 | bytes 24576
  56.2 39.8 %all-gather.6.cloned.1.call-done = bf16[3072,1536]{1,0:T(8,128)(2,1)} async-done(((bf16[96,1536]{1,0:T(8,128)(2,1)}), bf16[3072,1536]{1,0:T(8,128)(2,1)}) %all-gather.6.cloned.1.call-update) | async-done | bytes 9437200 | tf_op jit(solution)/shard_map/all_gather | solution.py:118
  96.1 5.5 fusion.46
  101.6 1.6 copy-done.21
  106.8 2.7 collective-permute-start
  109.4 9.5 collective-permute-done
  119.0 8.5 collective-permute-start.1
  127.5 41.2 %collective-permute-done.1 = bf16[512,1536]{1,0:T(8,128)(2,1)S(1)} collective-permute-done((bf16[512,1536]{1,0:T(8,128)(2,1)S(1)}, bf16[512,1536]{1,0:T(8,128)(2,1)S(1)}, u32[]{:S(2)}, u32[]{:S(2)}) %collective-permute-start.1) | collective-permute-done | bytes 1572896 | tf_op jit(solution)/shard_map/ppermute | solution.py:26
  168.9 2.8 collective-permute-start.2
  171.7 71.0 %collective-permute-done.2 = bf16[1024,1536]{1,0:T(8,128)(2,1)S(1)} collective-permute-done((bf16[1024,1536]{1,0:T(8,128)(2,1)S(1)}, bf16[1024,1536]{1,0:T(8,128)(2,1)S(1)}, u32[]{:S(2)}, u32[]{:S(2)}) %collective-permute-start.2) | collective-permute-done | bytes 3145760 | tf_op jit(solution)/shard_map/ppermute | solution.py:26
  248.0 2.1 constant_dynamic-update-slice_fusion.2
  250.1 136.4 %collective-permute-done.3 = bf16[2048,1536]{1,0:T(8,128)(2,1)} collective-permute-done((bf16[2048,1536]{1,0:T(8,128)(2,1)S(1)}, bf16[2048,1536]{1,0:T(8,128)(2,1)}, u32[]{:S(2)}, u32[]{:S(2)}) %collective-permute-start.3) | collective-permute-done | bytes 6291488 | tf_op jit(solution)/shard_map/ppermute | solution.py:26
  386.6 8.2 constant_dynamic-update-slice_fusion.1
  396.5 2.7 slice.91
  399.1 3.0 copy.66
  402.1 1.6 subtract_convert_fusion.1
  404.7 3.8 fusion.71
  408.5 2.8 copy.65
  411.3 2.6 copy.64
  413.8 4.3 fusion.19
  418.2 4.0 fusion.20
  422.2 4.9 fusion.37
  427.1 261.1 %all-gather.10.cloned.1.call-done = bf16[1536,1536]{1,0:T(8,128)(2,1)} async-done(((bf16[48,1536]{1,0:T(8,128)(2,1)}), bf16[1536,1536]{1,0:T(8,128)(2,1)}) %all-gather.10.cloned.1.call-update) | async-done | bytes 4718608 | tf_op jit(solution)/shard_map/all_gather | solution.py:119
  688.2 5.4 multiply_reduce_fusion.3
  693.6 264.0 %collective-permute-done.4 = bf16[4096,1536]{1,0:T(8,128)(2,1)} collective-permute-done((bf16[4096,1536]{1,0:T(8,128)(2,1)}, bf16[4096,1536]{1,0:T(8,128)(2,1)}, u32[]{:S(2)}, u32[]{:S(2)}) %collective-permute-start.4) | collective-permute-done | bytes 12582944 | tf_op jit(solution)/shard_map/ppermute | solution.py:26
  957.6 10.6 constant_dynamic-update-slice_fusion.12
  971.5 1.9 constant_dynamic-update-slice_fusion.8
  973.4 5.9 constant_dynamic-update-slice_fusion.7
  979.3 10.6 constant_dynamic-update-slice_fusion.6
  990.0 14.9 fusion.17
  1004.8 26.0 %all-gather.12.cloned.1.call-done = bf16[1536,4096]{1,0:T(8,128)(2,1)} async-done(((bf16[48,4096]{1,0:T(8,128)(2,1)}), bf16[1536,4096]{1,0:T(8,128)(2,1)}) %all-gather.12.cloned.1.call-update) | async-done | bytes 12582928 | tf_op jit(solution)/shard_map/all_gather | solution.py:187
  1030.8 13.7 multiply_convert_fusion.1
  1044.5 141.7 %all-gather.14.cloned.1.call-done = bf16[8192,1536]{1,0:T(8,128)(2,1)} async-done(((bf16[256,1536]{1,0:T(8,128)(2,1)}), bf16[8192,1536]{1,0:T(8,128)(2,1)}) %all-gather.14.cloned.1.call-update) | async-done | bytes 25165840 | tf_op jit(solution)/shard_map/all_gather | solution.py:197
  1186.2 13.7 multiply_reduce_fusion
  1205.4 59.4 %while.15 = (s32[]{:T(128)}, f32[256,8,2,96]{0,3,2,1:T(8,128)}, bf16[2,512,1536]{2,1,0:T(8,128)(2,1)}, s32[2]{0:T(128)S(1)}, bf16[1024,1536]{1,0:T(8,128)(2,1)},...) while((s32[]{:T(128)}, f32[256,8,2,96]{0,3,2,1:T(8,128)}, ...), condition=%wide.region_16.17_spmd.clone, body=%wide.region_13.16_spmd.clone.sunk | while | flops 2043966464 | bytes 127079328 | solution.py:273
  1209.3 4.6 fusion.125
  1214.2 5.5 fusion.128
  1219.7 1.9 copy-done
  1223.1 3.4 fusion.129
  1226.7 1.6 copy.103
  1228.2 2.8 constant_dynamic-update-slice_fusion.19
  1231.0 3.1 bitcast_add_fusion.2
  1238.7 4.6 fusion.125
  1243.6 5.5 fusion.128
  1249.2 1.9 copy-done
  1252.6 3.4 fusion.129
  1256.1 1.6 copy.103
  1257.7 2.8 constant_dynamic-update-slice_fusion.19
  1260.5 3.1 bitcast_add_fusion.2
  1264.8 4.6 copy.71
  1269.5 1.5 copy-done.14
  1271.2 10.9 convolution_bitcast_fusion
  1282.1 24.8 %copy.83 = f32[1536,4096]{1,0:T(8,128)} copy(f32[1536,4096]{0,1:T(8,128)} %convolution_bitcast_fusion) | data formatting | bytes 50331648
  1308.5 5.0 fusion.42
  1317.3 11.1 fusion.40
  1329.1 28.4 %fusion.25 = f32[8192,1536]{1,0:T(8,128)} fusion(bf16[256,4096]{1,0:T(8,128)(2,1)} %get-tuple-element.342, bf16[256,4096]{1,0:T(8,128)(2,1)} %get-tuple-element.341, f32[256,1536]{1,0:T(8,128)} %get-tuple-element.375, f32[1536]{0:T(1024)S(1)} %copy-done.33, f32[256]{0:T(256)} %copy-done.38), kind=kOutput, calls=%fused_computation.58 | convolution fusion | flops 6452019200 | bytes 56105984 | tf_op jit(solution)/shard_map/dot_general | solution.py:206
  1357.5 11.6 fusion.27
  1369.1 8.2 fusion.36
  1377.3 42.3 %all-reduce.4 = (f32[1536]{0:T(1024)S(1)}, f32[1536]{0:T(1024)S(1)}) all-reduce(f32[1536]{0:T(1024)} %get-tuple-element.305, f32[1536]{0:T(1024)} %get-tuple-element.303), channel_id=3, replica_groups=mesh['dp'=8,'ctx'=4] {'dp','ctx'}, use_global_device_ids=true, to_apply=%region_20.21.clone | all-reduce | flops 3072 | bytes 24576
  1421.4 3.0 fusion.33
  1424.4 132.3 %reduce-scatter.16.cloned.1.call-done = f32[48,4096]{1,0:T(8,128)} async-done(((f32[1536,4096]{1,0:T(8,128)}), f32[48,4096]{1,0:T(8,128)}) %reduce-scatter.16.cloned.1.call-update) | async-done | bytes 786448
  1556.7 142.2 %reduce-scatter.12.cloned.1.call-done = f32[48,1536]{1,0:T(8,128)} async-done(((f32[1536,1536]{1,0:T(8,128)}), f32[48,1536]{1,0:T(8,128)}) %reduce-scatter.12.cloned.1.call-update) | async-done | bytes 294928 | tf_op jit(solution)/shard_map/reduce_scatter | solution.py:96
  1698.9 212.8 %reduce-scatter.10.cloned.1.call-done = f32[96,1536]{1,0:T(8,128)} async-done(((f32[3072,1536]{1,0:T(8,128)}), f32[96,1536]{1,0:T(8,128)}) %reduce-scatter.10.cloned.1.call-update) | async-done | bytes 589840 | tf_op jit(solution)/shard_map/reduce_scatter | solution.py:95
  1911.7 435.2 %reduce-scatter.14.cloned.1.call-done = f32[256,1536]{1,0:T(8,128)} async-done(((f32[8192,1536]{1,0:T(8,128)}), f32[256,1536]{1,0:T(8,128)}) %reduce-scatter.14.cloned.1.call-update) | async-done | bytes 1572880 | tf_op jit(solution)/shard_map/reduce_scatter | solution.py:95
  (194 shorter events, 46.3 us)
Async XLA Ops:
  7.2 88.9 %all-gather.6.cloned.1.call-start = ((), (), s32[]{:S(2)}) async-start(), calls=%async_computation.5 | async-start | bytes 9732096 | tf_op jit(solution)/shard_map/all_gather | solution.py:118
  7.9 396.8 %all-gather.8.cloned.1.call-start = ((), (), s32[]{:S(2)}) async-start(), calls=%async_computation.6 | async-start | bytes 3932160 | tf_op jit(solution)/shard_map/all_gather | solution.py:163
  53.2 48.4 %copy-start.30 = (f32[1536]{0:T(1024)}, f32[1536]{0:T(1024)S(1)}, u32[]{:S(2)}) copy-start(f32[1536]{0:T(1024)S(1)} %get-tuple-element.337) | copy-start | bytes 18436
  53.2 1146.7 %copy-start.32 = (f32[1536]{0:T(1024)}, f32[1536]{0:T(1024)S(1)}, u32[]{:S(2)}) copy-start(f32[1536]{0:T(1024)S(1)} %get-tuple-element.338) | copy-start | bytes 18436
  56.0 45.6 %copy-start.35 = (f32[256]{0:T(256)}, f32[256]{0:T(256)S(1)}, u32[]{:S(2)}) copy-start(f32[256]{0:T(256)S(1)} %get-tuple-element.369) | copy-start | bytes 3076
  56.2 345.9 %copy-start.25 = (f32[256,48]{0,1:T(8,128)}, f32[256,48]{0,1:T(8,128)S(1)}, u32[]{:S(2)}) copy-start(f32[256,48]{0,1:T(8,128)S(1)} %get-tuple-element.366) | copy-start | bytes 147460
  56.2 345.9 %copy-start.27 = (f32[256,48]{0,1:T(8,128)}, f32[256,48]{0,1:T(8,128)S(1)}, u32[]{:S(2)}) copy-start(f32[256,48]{0,1:T(8,128)S(1)} %get-tuple-element.367) | copy-start | bytes 147460
  101.6 1.6 copy-start.21
  103.5 3.2 copy-start.5
  104.8 583.4 %all-gather.10.cloned.1.call-start = ((), (), s32[]{:S(2)}) async-start(), calls=%async_computation.7 | async-start | bytes 4866048 | tf_op jit(solution)/shard_map/all_gather | solution.py:119
  105.5 925.3 %all-gather.12.cloned.1.call-start = ((), (), s32[]{:S(2)}) async-start(), calls=%async_computation.8 | async-start | bytes 12976128 | tf_op jit(solution)/shard_map/all_gather | solution.py:187
  106.1 1080.1 %all-gather.14.cloned.1.call-start = ((), (), s32[]{:S(2)}) async-start(), calls=%async_computation.9 | async-start | bytes 25952256 | tf_op jit(solution)/shard_map/all_gather | solution.py:197
  106.7 1208.6 %reduce-scatter.8.cloned.1.call-start = ((), (), s32[]{:S(2)}) async-start(), calls=%async_computation.10 | async-start | bytes 3932160 | tf_op jit(solution)/shard_map/reduce_scatter | solution.py:278
  106.8 12.2 collective-permute-start
  118.9 126.7 %copy-start.8 = (bf16[256,1536]{1,0:T(8,128)(2,1)}, bf16[256,1536]{1,0:T(8,128)(2,1)S(1)}, u32[]{:S(2)}) copy-start(bf16[256,1536]{1,0:T(8,128)(2,1)S(1)} %collective-permute-done) | copy-start | bytes 2359300
  119.0 49.6 %collective-permute-start.1 = (bf16[512,1536]{1,0:T(8,128)(2,1)S(1)}, bf16[512,1536]{1,0:T(8,128)(2,1)S(1)}, u32[]{:S(2)}, u32[]{:S(2)}) collective-permute-start(bf16[512,1536]{1,0:T(8,128)(2,1)S(1)} %pad_maximum_fusion.5), channel_id=1, source_target_pairs={{0,30},{1,31},{2,0},{3,1},{4,2},{5,3},{6,4},{7,5},{8,6},{9,7},{10,... | collective-permute-start | bytes 4718600 | tf_op jit(solution)/shard_map/ppermute | solution.py:26
  168.9 73.8 %collective-permute-start.2 = (bf16[1024,1536]{1,0:T(8,128)(2,1)S(1)}, bf16[1024,1536]{1,0:T(8,128)(2,1)S(1)}, u32[]{:S(2)}, u32[]{:S(2)}) collective-permute-start(bf16[1024,1536]{1,0:T(8,128)(2,1)S(1)} %pad_maximum_fusion.2), channel_id=1, source_target_pairs={{0,28},{1,29},{2,30},{3,31},{4,0},{5,1},{6,2},{7,3},{8,4},{9,5},{1... | collective-permute-start | bytes 9437192 | tf_op jit(solution)/shard_map/ppermute | solution.py:26
  242.7 5.3 copy-start.6
  243.2 143.4 %collective-permute-start.3 = (bf16[2048,1536]{1,0:T(8,128)(2,1)S(1)}, bf16[2048,1536]{1,0:T(8,128)(2,1)}, u32[]{:S(2)}, u32[]{:S(2)}) collective-permute-start(bf16[2048,1536]{1,0:T(8,128)(2,1)S(1)} %pad_maximum_fusion), channel_id=1, source_target_pairs={{0,24},{1,25},{2,26},{3,27},{4,28},{5,29},{6,30},{7,31},{8,0},{9,1... | collective-permute-start | bytes 18874376 | tf_op jit(solution)/shard_map/ppermute | solution.py:26
  250.1 136.4 %copy-start.29 = (bf16[4096,1536]{1,0:T(8,128)(2,1)}, bf16[4096,1536]{1,0:T(8,128)(2,1)S(1)}, u32[]{:S(2)}) copy-start(bf16[4096,1536]{1,0:T(8,128)(2,1)S(1)} %get-tuple-element.346) | copy-start | bytes 37748740
  386.6 9.2 copy-start.40
  386.6 9.4 copy-start.34
  394.8 562.9 %collective-permute-start.4 = (bf16[4096,1536]{1,0:T(8,128)(2,1)}, bf16[4096,1536]{1,0:T(8,128)(2,1)}, u32[]{:S(2)}, u32[]{:S(2)}) collective-permute-start(bf16[4096,1536]{1,0:T(8,128)(2,1)} %get-tuple-element.344), channel_id=1, source_target_pairs={{0,16},{1,17},{2,18},{3,19},{4,20},{5,21},{6,22},{7,23},{8,24},{9,... | collective-permute-start | bytes 37748744 | tf_op jit(solution)/shard_map/ppermute | solution.py:26
  403.7 0.7 copy-start.15
  403.7 0.9 copy-start.16
  418.2 4.1 copy-start.22
  693.6 506.3 %copy-start.38 = (f32[256]{0:T(256)}, f32[256]{0:T(256)S(1)}, u32[]{:S(2)}) copy-start(f32[256]{0:T(256)S(1)} %get-tuple-element.371) | copy-start | bytes 3076
  957.6 11.7 copy-start.9
  968.3 3.2 copy-start.7
  979.3 10.6 copy-start.13
  990.0 40.9 %copy-start.19 = (bf16[256,1536]{1,0:T(8,128)(2,1)S(1)}, bf16[256,1536]{1,0:T(8,128)(2,1)}, u32[]{:S(2)}) copy-start(bf16[256,1536]{1,0:T(8,128)(2,1)} %param.19) | copy-start | bytes 2359300
  1186.2 15.3 slice-start
  1186.2 15.3 slice-start.1
  1200.3 1.1 copy-start.10
  1201.5 2.5 copy-start.17
  1214.2 8.9 copy-start.1
  1219.7 2.0 copy-start
  1228.2 2.8 copy-start.2
  1234.1 1.2 copy-start.3
  1243.6 8.9 copy-start.1
  1249.2 2.0 copy-start
  1257.7 2.8 copy-start.2
  1263.6 1.2 copy-start.3
  1269.4 1.6 copy-start.14
  1269.4 1.8 copy-start.20
  1269.5 287.2 %reduce-scatter.16.cloned.1.call-start = ((), (), s32[]{:S(2)}) async-start(), calls=%async_computation.14 | async-start | bytes 25952256
  1306.9 1.4 copy-start.11
  1306.9 1.6 copy-start.18
  1306.9 392.0 %reduce-scatter.12.cloned.1.call-start = ((), (), s32[]{:S(2)}) async-start(), calls=%async_computation.12 | async-start | bytes 9732096 | tf_op jit(solution)/shard_map/reduce_scatter | solution.py:96
  1313.5 1.4 copy-start.4
  1313.5 1.4 copy-start.26
  1313.5 1.4 copy-start.28
  1313.5 598.2 %reduce-scatter.10.cloned.1.call-start = ((), (), s32[]{:S(2)}) async-start(), calls=%async_computation.11 | async-start | bytes 19464192 | tf_op jit(solution)/shard_map/reduce_scatter | solution.py:95
  1315.1 2.1 copy-start.12
  1315.1 2.1 copy-start.31
  1315.2 2.1 copy-start.36
  1316.5 0.8 copy-start.23
  1328.4 0.7 copy-start.33
  1328.4 1018.6 %reduce-scatter.14.cloned.1.call-start = ((), (), s32[]{:S(2)}) async-start(), calls=%async_computation.13 | async-start | bytes 51904512 | tf_op jit(solution)/shard_map/reduce_scatter | solution.py:95
  1357.4 11.6 copy-start.24
  1357.5 11.6 copy-start.37
  1369.1 52.3 %copy-start.39 = (f32[256]{0:T(256)S(1)}, f32[256]{0:T(256)}, u32[]{:S(2)}) copy-start(f32[256]{0:T(256)} %get-tuple-element.368) | copy-start | bytes 3076
Sparse Core Ops, SparseCore 0:
  10.9 85.1 all-gather.5
  104.9 64.2 all-gather.7
  172.2 516.0 all-gather.9
  691.0 339.8 all-gather.11
  1033.6 152.6 all-gather.13
  1269.6 35.8 reduce-scatter.7
  1312.5 244.1 reduce-scatter.15
  1563.2 135.7 reduce-scatter.11
  1705.9 205.7 reduce-scatter.9
  1918.6 428.3 reduce-scatter.13
